TPU v7x, 32 devices: a whole 2x2x4 slice. The times are simulated.
32 devices in a mesh: ep: 32 (over z, y, x, core).
Axes of the slice: x: 2, y: 2, z: 4, core: 2. Of those that a mesh axis runs over, the one named last changes fastest.
Arguments:
- x_in: bfloat16 [12288, 2048], P('ep')
- route_idx: int32 [12288, 8], P('ep')
- gate_w: bfloat16 [12288, 8], P('ep')
- dy_in: bfloat16 [12288, 2048], P('ep')
- w_gate: bfloat16 [32, 2048, 1024], P('ep')
- w_up: bfloat16 [32, 2048, 1024], P('ep')
- w_down: bfloat16 [32, 1024, 2048], P('ep')
- hot_gate: bfloat16 [2048, 1024], replicated
- hot_up: bfloat16 [2048, 1024], replicated
- hot_down: bfloat16 [1024, 2048], replicated
Outputs:
- output 1: bfloat16 [12288, 2048], P('ep')
- output 2: bfloat16 [12288, 2048], P('ep')
- output 3: float32 [32, 2048, 1024], P('ep')
- output 4: float32 [32, 2048, 1024], P('ep')
- output 5: float32 [32, 1024, 2048], P('ep')
- output 6: float32 [2048, 1024], P(None, 'ep')
- output 7: float32 [2048, 1024], P(None, 'ep')
- output 8: float32 [1024, 2048], P('ep')
All inputs are finite; a program needn't handle non-finite values.
Results may differ from a plain program's by a relative error of at most 0.0107406.
Values are sent between devices in bfloat16 or wider.
A program may use at most 1 GiB of HBM per device.

v0:
```python
import jax
import jax.numpy as jnp
from jax import lax
from jax.experimental import pallas as pl
from jax.experimental.pallas import tpu as pltpu
from jax.sharding import PartitionSpec as P


BF16 = jnp.bfloat16
F32 = jnp.float32
CONTRACT_LAST = (((1,), (1,)), ((), ()))
CONTRACT_FIRST = (((0,), (0,)), ((), ()))


def dot(a, b, dims=(((1,), (0,)), ((), ()))):
    return lax.dot_general(a, b, dims, preferred_element_type=F32)


def silu_parts(pre_gate):
    sig_val = jax.nn.sigmoid(pre_gate)
    return pre_gate * sig_val, sig_val * (1.0 + pre_gate * (1.0 - sig_val))


def hot_grad_kernel(x_ref, dy_ref, gate_ref, mask_ref, wgu_ref, wd_ref, dgu_ref, dd_ref):
    half = wd_ref.shape[0]

    @pl.when(pl.program_id(0) == 0)
    def _():
        dgu_ref[...] = jnp.zeros_like(dgu_ref)
        dd_ref[...] = jnp.zeros_like(dd_ref)

    x_rows = x_ref[...]
    q_rows = (gate_ref[...] * dy_ref[...].astype(F32)).astype(BF16)
    chosen = mask_ref[...] > 0.0
    uv = dot(x_rows, wgu_ref[...])
    p_val = dot(q_rows, wd_ref[...], CONTRACT_LAST).astype(BF16).astype(F32)
    u_val, v_val = uv[:, :half], uv[:, half:]
    silu_val, silu_grad = silu_parts(u_val)
    hidden = jnp.where(chosen, silu_val * v_val, 0.0).astype(BF16)
    du = jnp.where(chosen, p_val * v_val * silu_grad, 0.0).astype(BF16)
    dv = jnp.where(chosen, p_val * silu_val, 0.0).astype(BF16)
    dgu_ref[...] += dot(jnp.concatenate([du, dv], axis=1), x_rows, CONTRACT_FIRST)
    dd_ref[...] += dot(hidden, q_rows, CONTRACT_FIRST)


def hot_grads(x_all, dy_all, gate_col, mask_col, wgu, wd, block=512):
    total, d_model = x_all.shape
    half = wd.shape[0]
    flops = 2 * total * d_model * (6 * half)
    return pl.pallas_call(
        hot_grad_kernel,
        grid=(total // block,),
        in_specs=[
            pl.BlockSpec((block, d_model), lambda i: (i, 0)),
            pl.BlockSpec((block, d_model), lambda i: (i, 0)),
            pl.BlockSpec((block, 1), lambda i: (i, 0)),
            pl.BlockSpec((block, 1), lambda i: (i, 0)),
            pl.BlockSpec((d_model, 2 * half), lambda i: (0, 0)),
            pl.BlockSpec((half, d_model), lambda i: (0, 0)),
        ],
        out_specs=[
            pl.BlockSpec((2 * half, d_model), lambda i: (0, 0)),
            pl.BlockSpec((half, d_model), lambda i: (0, 0)),
        ],
        out_shape=[jax.ShapeDtypeStruct((2 * half, d_model), F32), jax.ShapeDtypeStruct((half, d_model), F32)],
        cost_estimate=pl.CostEstimate(flops=flops, bytes_accessed=4 * total * d_model, transcendentals=0),
        compiler_params=pltpu.CompilerParams(dimension_semantics=("arbitrary",), vmem_limit_bytes=50 * 2**20),
        name="hot_grads",
    )(x_all, dy_all, gate_col, mask_col, wgu, wd)


def solution(mesh):
    n_dev = mesh.shape['ep']

    def local_step(x_loc, route_loc, gate_loc, dy_loc, w_gate, w_up, w_down, hot_gate, hot_up, hot_down):
        tok, top_k = route_loc.shape
        d_model = x_loc.shape[1]
        d_ff = w_gate.shape[2]
        total = n_dev * tok
        slot_cap = min(tok, 2 * tok * top_k // n_dev)
        n_rows = n_dev * slot_cap
        me = lax.axis_index('ep')

        meta = jnp.concatenate([route_loc.T.astype(F32), gate_loc.T.astype(F32)], axis=0)
        meta_all = lax.all_gather(meta, 'ep')
        x_all = lax.all_gather(x_loc, 'ep', tiled=True)
        dy_all = lax.all_gather(dy_loc, 'ep', tiled=True)
        route_all, gate_all = meta_all[:, :top_k], meta_all[:, top_k:]

        mine = route_all == me.astype(F32)
        has = jnp.any(mine, axis=1)
        gate_mine = jnp.sum(jnp.where(mine, gate_all, 0.0), axis=1)
        tri = (jnp.arange(tok)[:, None] <= jnp.arange(tok)[None, :]).astype(BF16)
        order = jnp.where(has, dot(has.astype(BF16), tri), 0.0)[:, None, :]
        match = order == jnp.arange(1, slot_cap + 1).astype(F32)[None, :, None]

        def pick_rows(picker, rows):
            picked = lax.dot_general(picker.astype(BF16), rows.reshape(n_dev, tok, d_model), (((2,), (1,)), ((0,), (0,))), preferred_element_type=F32)
            return picked.astype(BF16).reshape(n_rows, d_model)

        hot_all = route_all == float(n_dev)
        hot_mask = jnp.any(hot_all, axis=1).astype(F32).reshape(total, 1)
        hot_gate_w = jnp.sum(jnp.where(hot_all, gate_all, 0.0), axis=1).reshape(total, 1)
        own_hot = route_loc == n_dev
        own_hot_mask = jnp.any(own_hot, axis=1)[:, None]
        own_hot_gate = jnp.sum(jnp.where(own_hot, gate_loc.astype(F32), 0.0), axis=1)[:, None]

        one_hot = route_loc[:, :, None] == jnp.arange(n_dev, dtype=jnp.int32)[None, None, :]
        own_has = jnp.any(one_hot, axis=1)
        own_gate = jnp.sum(jnp.where(one_hot, gate_loc.astype(F32)[:, :, None], 0.0), axis=1)
        rank = jnp.where(own_has, dot(tri, own_has.astype(BF16), CONTRACT_FIRST) - 1.0, -1.0)
        col = jnp.arange(n_rows, dtype=jnp.int32)
        widen = (jnp.arange(n_dev)[:, None] == col[None, :] // slot_cap).astype(BF16)
        back_match = dot(rank.astype(BF16), widen) == (col % slot_cap).astype(F32)[None, :]
        back_ones = back_match.astype(BF16)
        back_gates = jnp.where(back_match, dot(own_gate.astype(BF16), widen), 0.0).astype(BF16)

        def give_back(rows):
            return lax.all_to_all(rows.astype(BF16), 'ep', 0, 0, tiled=True)

        wg, wu, wd = w_gate[0], w_up[0], w_down[0]
        x_rows = pick_rows(match, x_all)
        u_val = dot(x_rows, wg)
        v_val = dot(x_rows, wu)
        hidden = (silu_parts(u_val)[0] * v_val).astype(BF16)
        hidden, u_val, v_val = lax.optimization_barrier((hidden, u_val, v_val))
        o_rows = dot(hidden, wd).astype(BF16)
        back_o = give_back(o_rows)
        gate_late, _ = lax.optimization_barrier((gate_mine, o_rows))

        q_rows = pick_rows(jnp.where(match, gate_late[:, None, :], 0.0), dy_all)
        p_val = dot(q_rows, wd, CONTRACT_LAST).astype(BF16).astype(F32)
        silu_val, silu_grad = silu_parts(u_val)
        du = (p_val * v_val * silu_grad).astype(BF16)
        dv = (p_val * silu_val).astype(BF16)
        r_rows = (dot(du, wg, CONTRACT_LAST) + dot(dv, wu, CONTRACT_LAST)).astype(BF16)
        r_rows, back_o = lax.optimization_barrier((r_rows, back_o))
        back_r = give_back(r_rows)
        grad_gate = dot(x_rows, du, CONTRACT_FIRST)
        grad_up = dot(x_rows, dv, CONTRACT_FIRST)
        grad_down = dot(hidden, q_rows, CONTRACT_FIRST)

        hu = dot(x_loc, hot_gate)
        hv = dot(x_loc, hot_up)
        h_silu, h_silu_grad = silu_parts(hu)
        h_hidden = (h_silu * hv).astype(BF16)
        h_out = dot(h_hidden, hot_down).astype(BF16)
        h_q = (own_hot_gate * dy_loc.astype(F32)).astype(BF16)
        h_p = dot(h_q, hot_down, CONTRACT_LAST).astype(BF16).astype(F32)
        h_du = jnp.where(own_hot_mask, h_p * hv * h_silu_grad, 0.0).astype(BF16)
        h_dv = jnp.where(own_hot_mask, h_p * h_silu, 0.0).astype(BF16)
        h_r = (dot(h_du, hot_gate, CONTRACT_LAST) + dot(h_dv, hot_up, CONTRACT_LAST)).astype(BF16)
        y_hot = jnp.where(own_hot_mask, own_hot_gate * h_out.astype(F32), 0.0)

        part = d_ff // n_dev
        pad = ((0, 0), (0, 128 - part))
        g_part = jnp.pad(lax.dynamic_slice_in_dim(hot_gate, me * part, part, 1), pad)
        u_part = jnp.pad(lax.dynamic_slice_in_dim(hot_up, me * part, part, 1), pad)
        d_part = jnp.pad(lax.dynamic_slice_in_dim(hot_down, me * part, part, 0), ((0, 128 - part), (0, 0)))
        dgu, dd = hot_grads(x_all, dy_all, hot_gate_w, hot_mask, jnp.concatenate([g_part, u_part], axis=1), d_part)
        hot_dgate = dgu[:part].T
        hot_dup = dgu[128:128 + part].T
        hot_ddown = dd[:part]

        y_loc = dot(back_gates, back_o) + y_hot
        dx_loc = dot(back_ones, back_r) + h_r.astype(F32)
        return (y_loc.astype(BF16), dx_loc.astype(BF16), grad_gate[None], grad_up[None], grad_down[None],
                hot_dgate, hot_dup, hot_ddown)

    row_spec = P('ep', None)
    expert_spec = P('ep', None, None)
    whole_spec = P(None, None)
    return jax.shard_map(local_step, mesh=mesh, in_specs=(row_spec, row_spec, row_spec, row_spec, expert_spec, expert_spec, expert_spec, whole_spec, whole_spec, whole_spec), out_specs=(row_spec, row_spec, expert_spec, expert_spec, expert_spec, P(None, 'ep'), P(None, 'ep'), P('ep', None)), check_vma=False)
```

profile of v0, /device:TPU:6, one launch (start us, length us, event | category | flops | bytes accessed | tf_op | source)
XLA Modules:
  0.0 1676.8 jit_solution(1773673637851730696)
XLA Ops:
  7.2 0.0 all-gather.4.cloned.1.call-start
  7.2 0.7 all-gather.4.cloned.1.call-update
  7.9 0.0 all-gather.6.cloned.1.call-start
  7.9 0.7 all-gather.6.cloned.1.call-update
  8.7 0.7 convert_bitcast_fusion.1
  9.4 1.3 fusion.72
  10.7 37.7 %all-gather = f32[512,384]{1,0:T(8,128)S(1)} all-gather(f32[16,384]{1,0:T(8,128)S(1)} %pad_maximum_fusion), channel_id=2, replica_groups=mesh['ep'=32] {'ep'}, dimensions={0}, use_global_device_ids=true | all-gather | bytes 811008 | tf_op jit(solution)/shard_map/all_gather | solution.py:85
  48.3 0.8 fusion.70
  49.1 0.9 select_reduce_fusion
  50.0 0.1 reduce_or.37
  50.1 0.0 copy-start.7
  50.1 0.2 convolution_select_fusion
  50.3 0.0 copy-start.2
  50.3 238.2 %all-gather.4.cloned.1.call-done.x_ref = bf16[12288,2048]{1,0:T(8,128)(2,1)} async-done(((bf16[384,2048]{1,0:T(8,128)(2,1)}), bf16[12288,2048]{1,0:T(8,128)(2,1)}) %all-gather.4.cloned.1.call-update) | async-done | bytes 50331664 | tf_op jit(solution)/shard_map/all_gather | solution.py:86
  288.6 27.2 %convolution_convert_fusion.1 = bf16[32,192,2048]{2,1,0:T(8,128)(2,1)} fusion(bf16[32,384,2048]{2,1,0:T(8,128)(2,1)} %bitcast.78, f32[32,384]{1,0:T(8,128)S(1)} %convolution_select_fusion, f32[192]{0:T(256)S(1)} %add_convert_fusion.4), kind=kOutput, calls=%fused_computation.9 | convolution fusion | flops 9678618624 | bytes 75547392 | tf_op jit(solution)/shard_map/dot_general | solution.py:98
  315.8 0.0 copy-done.7
  315.8 33.0 %fusion.19 = f32[6144,1024]{1,0:T(8,128)} fusion(bf16[6144,2048]{1,0:T(8,128)(2,1)} %bitcast.80, bf16[1,2048,1024]{2,1,0:T(8,128)(2,1)} %param.14), kind=kOutput, calls=%fused_computation.33 | convolution fusion | flops 25769803776 | bytes 54525952 | tf_op jit(solution)/shard_map/dot_general | solution.py:16
  348.8 40.2 %multiply_convert_fusion = (bf16[6144,1024]{1,0:T(8,128)(2,1)}, f32[6144,1024]{1,0:T(8,128)}) fusion(f32[6144,1024]{1,0:T(8,128)} %fusion.19, bf16[6144,2048]{1,0:T(8,128)(2,1)} %bitcast.81, bf16[1,2048,1024]{2,1,0:T(8,128)(2,1)} %param.15), kind=kOutput, calls=%fused_computation.7 | convolution fusion | flops 25807552512 | bytes 92274688 | tf_op jit(solution)/shard_map/dot_general | solution.py:16
  389.1 34.8 %convolution_convert_fusion = bf16[6144,2048]{1,0:T(8,128)(2,1)} fusion(bf16[6144,1024]{1,0:T(8,128)(2,1)} %get-tuple-element.16, bf16[1,1024,2048]{2,1,0:T(8,128)(2,1)S(1)} %copy-done.23), kind=kOutput, calls=%fused_computation.8 | convolution fusion | flops 25782386688 | bytes 41943040 | tf_op jit(solution)/shard_map/dot_general | solution.py:16
  423.9 5.8 all-to-all-start
  429.7 341.8 %all-gather.6.cloned.1.call-done.dy_ref = bf16[12288,2048]{1,0:T(8,128)(2,1)} async-done(((bf16[384,2048]{1,0:T(8,128)(2,1)}), bf16[12288,2048]{1,0:T(8,128)(2,1)}) %all-gather.6.cloned.1.call-update) | async-done | bytes 50331664 | tf_op jit(solution)/shard_map/all_gather | solution.py:87
  771.5 26.9 %convolution_convert_fusion.2 = bf16[32,192,2048]{2,1,0:T(8,128)(2,1)} fusion(bf16[32,384,2048]{2,1,0:T(8,128)(2,1)} %bitcast.79, bf16[32,384]{1,0:T(8,128)(2,1)S(1)} %copy-done.6, f32[32,384]{1,0:T(8,128)S(1)} %copy-done.3, f32[192]{0:T(256)S(1)} %copy-done.8), kind=kOutput, calls=%fused_computation.10 | convolution fusion | flops 9680977920 | bytes 75571968 | tf_op jit(solution)/shard_map/dot_general | solution.py:98
  798.4 42.9 %fusion.1 = (bf16[6144,1024]{1,0:T(8,128)(2,1)}, bf16[6144,1024]{1,0:T(8,128)(2,1)}) fusion(f32[6144,1024]{1,0:T(8,128)} %get-tuple-element.18, f32[6144,1024]{1,0:T(8,128)} %fusion.19, bf16[6144,2048]{1,0:T(8,128)(2,1)} %bitcast.86, bf16[1,1024,2048]{2,1,0:T(8,128)(2,1)} %param.16), kind=kOutput, calls=%fused_computation.4 | convolution fusion | flops 25845301248 | bytes 104857600 | tf_op jit(solution)/shard_map/dot_general | solution.py:16
  841.3 34.9 %fusion.17 = f32[6144,2048]{1,0:T(8,128)} fusion(bf16[6144,1024]{1,0:T(8,128)(2,1)} %get-tuple-element.37, bf16[1,2048,1024]{2,1,0:T(8,128)(2,1)} %param.14), kind=kOutput, calls=%fused_computation.31 | convolution fusion | flops 25769803776 | bytes 67108864 | tf_op jit(solution)/shard_map/dot_general | solution.py:16
  876.2 45.1 %add_convert_fusion = bf16[6144,2048]{1,0:T(8,128)(2,1)} fusion(f32[6144,2048]{1,0:T(8,128)} %fusion.17, bf16[1,2048,1024]{2,1,0:T(8,128)(2,1)} %param.15, bf16[6144,1024]{1,0:T(8,128)(2,1)} %get-tuple-element.38, f32[6144,1024]{1,0:T(8,128)} %fusion.19), kind=kOutput, calls=%fused_computation | convolution fusion | flops 25839009792 | bytes 117440512 | tf_op jit(solution)/shard_map/dot_general | solution.py:16
  921.3 181.3 %all-to-all-done = bf16[32,192,2048]{2,1,0:T(8,128)(2,1)} async-done(((bf16[32,192,2048]{2,1,0:T(8,128)(2,1)}), bf16[32,192,2048]{2,1,0:T(8,128)(2,1)}, u32[]{:S(2)}, u32[]{:S(2)}) %all-to-all-start) | async-done | bytes 25165856 | tf_op jit(solution)/shard_map/all_to_all | solution.py:119
  1102.6 4.4 all-to-all-start.1
  1106.9 0.1 copy.26
  1107.0 0.1 copy.28
  1107.1 4.0 copy.29
  1111.0 3.9 copy.27
  1115.0 1.0 constant_dynamic-slice_fusion
  1116.2 0.0 copy-start.21
  1116.2 0.0 copy-done.17
  1116.2 0.1 fusion.46
  1116.3 0.6 select_reduce_fusion.2
  1116.9 1.6 constant_dynamic-slice_fusion.1
  1118.5 0.2 fusion.34.wgu_ref
  1118.7 0.0 copy-start.10
  1118.7 5.3 fusion.73
  1124.0 0.0 copy-done.10
  1124.0 3.0 fusion.74
  1127.0 0.0 copy-done.18
  1127.0 2.7 fusion.31
  1129.7 3.1 convolution_compare_fusion
  1132.8 0.0 copy-done.25
  1132.8 5.8 convolution_convert_fusion.4
  1138.6 0.0 copy-done.26
  1138.6 0.0 copy-start.11
  1138.6 2.1 fusion.36
  1140.8 0.0 copy-done.11
  1140.8 3.1 add_convert_fusion.2
  1143.9 58.4 %hot_grads.1 = (f32[256,2048]{1,0:T(8,128)}, f32[128,2048]{1,0:T(8,128)S(1)}) custom-call(bf16[12288,2048]{1,0:T(8,128)(2,1)} %all-gather.4.cloned.1.call-done.x_ref, bf16[12288,2048]{1,0:T(8,128)(2,1)} %all-gather.6.cloned.1.call-done.dy_ref, f32[12288,1]{1,0:T(8,128)} %bitcast.89, f32[12288,1]{1,0:T(8,128)} %bitcast.88, ...), custom_call_target="tpu_custom_call" | custom-call | flops 38654705664 | bytes 100663296 | tf_op jit(solution)/shard_map/hot_grads/pallas_call | solution.py:50
  1202.3 0.7 slice.19
  1203.1 1.9 slice_bitcast_fusion
  1204.9 34.6 %convolution_bitcast_fusion = f32[1,1024,2048]{2,1,0:T(8,128)} fusion(bf16[6144,1024]{1,0:T(8,128)(2,1)} %get-tuple-element.16, bf16[6144,2048]{1,0:T(8,128)(2,1)} %bitcast.87), kind=kOutput, calls=%fused_computation.23 | convolution fusion | flops 25769803776 | bytes 46137344 | tf_op jit(solution)/shard_map/dot_general | solution.py:16
  1239.5 0.0 slice-done.2
  1239.5 30.8 %convolution_bitcast_fusion.2 = f32[1,2048,1024]{2,1,0:T(8,128)} fusion(bf16[6144,2048]{1,0:T(8,128)(2,1)} %bitcast.82, bf16[6144,1024]{1,0:T(8,128)(2,1)S(1)} %bitcast.96), kind=kOutput, calls=%fused_computation.25 | convolution fusion | flops 25769803776 | bytes 46137344 | tf_op jit(solution)/shard_map/dot_general | solution.py:16
  1270.3 0.0 copy-start.24
  1270.3 37.2 %convolution_bitcast_fusion.1 = f32[1,2048,1024]{2,1,0:T(8,128)} fusion(bf16[6144,2048]{1,0:T(8,128)(2,1)} %bitcast.83, bf16[6144,1024]{1,0:T(8,128)(2,1)} %get-tuple-element.38, f32[6144,1024]{1,0:T(8,128)} %fusion.19), kind=kOutput, calls=%fused_computation.24 | convolution fusion | flops 25813843968 | bytes 71303168 | tf_op jit(solution)/shard_map/dot_general | solution.py:16
  1307.5 0.0 copy-start.28
  1307.5 18.9 %add_convert_fusion.3 = bf16[384,2048]{1,0:T(8,128)(2,1)} fusion(bf16[384,2048]{1,0:T(8,128)(2,1)S(1)} %copy-done.24, bf16[6144,2048]{1,0:T(8,128)(2,1)} %bitcast.11, pred[384,6144]{1,0:T(32,128)(4,1)} %convolution_compare_fusion, f32[384]{0:T(512)S(1)} %copy-done.20, pred[384]{0:T(512)(128)(4,1)S(1)} %copy-done.22, s32[6144]{0:T(1024)S(1)} %copy-done.15, ...), kind=kOutput, calls=%fused_computation.38 | convolution fusion | flops 9823518720 | bytes 30721920 | tf_op jit(solution)/shard_map/dot_general | solution.py:16
  1326.5 326.5 %all-to-all-done.1 = bf16[32,192,2048]{2,1,0:T(8,128)(2,1)} async-done(((bf16[32,192,2048]{2,1,0:T(8,128)(2,1)}), bf16[32,192,2048]{2,1,0:T(8,128)(2,1)}, u32[]{:S(2)}, u32[]{:S(2)}) %all-to-all-start.1) | async-done | bytes 25165856 | tf_op jit(solution)/shard_map/all_to_all | solution.py:119
  1653.0 16.5 add_convert_fusion.1
  (58 shorter events, 0.2 us)
Async XLA Ops:
  7.2 281.4 %all-gather.4.cloned.1.call-start = ((), (), s32[]{:S(2)}) async-start(), calls=%async_computation.2 | async-start | bytes 51904512 | tf_op jit(solution)/shard_map/all_gather | solution.py:86
  7.9 763.6 %all-gather.6.cloned.1.call-start = ((), (), s32[]{:S(2)}) async-start(), calls=%async_computation.3 | async-start | bytes 51904512 | tf_op jit(solution)/shard_map/all_gather | solution.py:87
  50.1 265.7 %copy-start.7 = (f32[192]{0:T(256)}, f32[192]{0:T(256)S(1)}, u32[]{:S(2)}) copy-start(f32[192]{0:T(256)S(1)} %add_convert_fusion.4) | copy-start | bytes 2308
  50.3 265.5 %copy-start.2 = (f32[32,384]{1,0:T(8,128)}, f32[32,384]{1,0:T(8,128)S(1)}, u32[]{:S(2)}) copy-start(f32[32,384]{1,0:T(8,128)S(1)} %convolution_select_fusion) | copy-start | bytes 147460
  348.8 40.2 %copy-start.23 = (bf16[1,1024,2048]{2,1,0:T(8,128)(2,1)S(1)}, bf16[1,1024,2048]{2,1,0:T(8,128)(2,1)}, u32[]{:S(2)}) copy-start(bf16[1,1024,2048]{2,1,0:T(8,128)(2,1)} %param.16) | copy-start | bytes 12582916
  423.9 347.7 %copy-start.3 = (f32[32,384]{1,0:T(8,128)S(1)}, f32[32,384]{1,0:T(8,128)}, u32[]{:S(2)}) copy-start(f32[32,384]{1,0:T(8,128)} %copy-done.2) | copy-start | bytes 147460
  423.9 347.7 %copy-start.6 = (bf16[32,384]{1,0:T(8,128)(2,1)S(1)}, bf16[32,384]{1,0:T(8,128)(2,1)}, u32[]{:S(2)}) copy-start(bf16[32,384]{1,0:T(8,128)(2,1)} %get-tuple-element.17) | copy-start | bytes 73732
  423.9 347.7 %copy-start.8 = (f32[192]{0:T(256)S(1)}, f32[192]{0:T(256)}, u32[]{:S(2)}) copy-start(f32[192]{0:T(256)} %copy-done.7) | copy-start | bytes 2308
  423.9 678.7 %all-to-all-start = ((bf16[32,192,2048]{2,1,0:T(8,128)(2,1)}), bf16[32,192,2048]{2,1,0:T(8,128)(2,1)}, u32[]{:S(2)}, u32[]{:S(2)}) async-start(bf16[32,192,2048]{2,1,0:T(8,128)(2,1)} %bitcast.85), calls=%async_computation | async-start | bytes 50331648 | tf_op jit(solution)/shard_map/all_to_all | solution.py:119
  1102.6 4.4 copy-start.5
  1102.6 4.4 copy-start.13
  1102.6 550.4 %all-to-all-start.1 = ((bf16[32,192,2048]{2,1,0:T(8,128)(2,1)}), bf16[32,192,2048]{2,1,0:T(8,128)(2,1)}, u32[]{:S(2)}, u32[]{:S(2)}) async-start(bf16[32,192,2048]{2,1,0:T(8,128)(2,1)} %bitcast.84), calls=%async_computation.1 | async-start | bytes 50331648 | tf_op jit(solution)/shard_map/all_to_all | solution.py:119
  1111.0 5.1 copy-start.4
  1111.0 5.1 copy-start.17
  1111.0 5.2 copy-start.12
  1115.0 3.7 copy-start
  1116.1 13.6 copy-start.14
  1116.2 24.6 %copy-start.21 = (pred[384]{0:T(512)(128)(4,1)}, pred[384]{0:T(512)(128)(4,1)S(1)}, u32[]{:S(2)}) copy-start(pred[384]{0:T(512)(128)(4,1)S(1)} %get-tuple-element.28) | copy-start | bytes 1156
  1116.2 10.8 copy-start.19
  1118.7 5.3 copy-start.10
  1124.0 3.0 copy-start.1
  1124.0 3.0 copy-start.18
  1129.7 3.1 copy-start.25
  1132.8 5.8 copy-start.9
  1132.8 5.8 copy-start.26
  1132.8 5.8 copy-start.27
  1138.6 2.2 copy-start.11
  1143.9 95.6 %slice-start = ((s8[12582912]{0:T(1024)(128)(4,1)}), s8[4194304]{0:T(1024)(128)(4,1)S(1)}, s32[]{:S(2)}) async-start(s8[12582912]{0:T(1024)(128)(4,1)} %bitcast.95), calls=%async_computation.4 | async-start | bytes 8388608
  1143.9 95.6 %slice-start.1 = ((s8[12582912]{0:T(1024)(128)(4,1)}), s8[4194304]{0:T(1024)(128)(4,1)S(1)}, s32[]{:S(2)}) async-start(s8[12582912]{0:T(1024)(128)(4,1)} %bitcast.95), calls=%async_computation.5 | async-start | bytes 8388608
  1204.9 34.6 %slice-start.2 = ((s8[12582912]{0:T(1024)(128)(4,1)}), s8[4194304]{0:T(1024)(128)(4,1)S(1)}, s32[]{:S(2)}) async-start(s8[12582912]{0:T(1024)(128)(4,1)} %bitcast.95), calls=%async_computation.6 | async-start | bytes 8388608
  1270.3 37.2 %copy-start.15 = (s32[6144]{0:T(1024)S(1)}, s32[6144]{0:T(1024)}, u32[]{:S(2)}) copy-start(s32[6144]{0:T(1024)} %copy-done.14) | copy-start | bytes 73732
  1270.3 37.2 %copy-start.16 = (bf16[384,32]{0,1:T(8,128)(2,1)S(1)}, bf16[384,32]{0,1:T(8,128)(2,1)}, u32[]{:S(2)}) copy-start(bf16[384,32]{0,1:T(8,128)(2,1)} %select_reduce_fusion.2) | copy-start | bytes 73732
  1270.3 37.2 %copy-start.20 = (f32[384]{0:T(512)S(1)}, f32[384]{0:T(512)}, u32[]{:S(2)}) copy-start(f32[384]{0:T(512)} %copy-done.19) | copy-start | bytes 4612
  1270.3 37.2 %copy-start.22 = (pred[384]{0:T(512)(128)(4,1)S(1)}, pred[384]{0:T(512)(128)(4,1)}, u32[]{:S(2)}) copy-start(pred[384]{0:T(512)(128)(4,1)} %copy-done.21) | copy-start | bytes 1156
  1270.3 37.2 %copy-start.24 = (bf16[384,2048]{1,0:T(8,128)(2,1)S(1)}, bf16[384,2048]{1,0:T(8,128)(2,1)}, u32[]{:S(2)}) copy-start(bf16[384,2048]{1,0:T(8,128)(2,1)} %convolution_convert_fusion.4) | copy-start | bytes 4718596
  1307.5 345.5 %copy-start.28 = (bf16[384,2048]{1,0:T(8,128)(2,1)S(1)}, bf16[384,2048]{1,0:T(8,128)(2,1)}, u32[]{:S(2)}) copy-start(bf16[384,2048]{1,0:T(8,128)(2,1)} %add_convert_fusion.2) | copy-start | bytes 4718596
Sparse Core Ops, SparseCore 0:
  10.8 277.6 all-gather.3
  291.4 480.0 all-gather.5
where the time goes:
time: 1700 us; the launch traced here: 1680 us
  waiting for transfers between devices  1090 us (64%)
  matrix products  448 us (26%)
  Pallas kernels  58.4 us (3%)
  blocking collectives  37.7 us (2%)
    all_to_all x2, waiting for transfers between devices, give_back(): return lax.all_to_all(rows.astype(BF16), 'ep', 0, 0, tiled=True)  508 us
    dot_general x19, matrix products, dot(): return lax.dot_general(a, b, dims, preferred_element_type=F32)  394 us
    all_gather x1, waiting for transfers between devices, local_step(): dy_all = lax.all_gather(dy_loc, 'ep', tiled=True)  342 us
    all_gather x1, waiting for transfers between devices, local_step(): x_all = lax.all_gather(x_loc, 'ep', tiled=True)  238 us
    pallas_call x1, Pallas kernels, hot_grads(): pl.pallas_call(hot_grad_kernel, grid=(total // block,), in_specs=[pl.Bloc...  58.4 us
    dot_general x2, matrix products, pick_rows(): lax.dot_general(picker.astype(BF16), rows.reshape(n_dev, tok, d_model), (...  54.1 us
    all_gather x1, blocking collectives, local_step(): meta_all = lax.all_gather(meta, 'ep')  37.7 us
  transfers between devices with their start and end apart: 4, of which 4 were waited for; matrix products, arithmetic and copies ran while one was open for 27% of the time, Pallas kernels for 3%

commit v1 on v0

--- a/solution.py
+++ b/solution.py
@@ -71,6 +71,8 @@
 
 def solution(mesh):
     n_dev = mesh.shape['ep']
+    n_z = 4
+    shifts = (2, 1, 3, 0)
 
     def local_step(x_loc, route_loc, gate_loc, dy_loc, w_gate, w_up, w_down, hot_gate, hot_up, hot_down):
         tok, top_k = route_loc.shape
@@ -105,18 +107,36 @@
         own_hot_mask = jnp.any(own_hot, axis=1)[:, None]
         own_hot_gate = jnp.sum(jnp.where(own_hot, gate_loc.astype(F32), 0.0), axis=1)[:, None]
 
-        one_hot = route_loc[:, :, None] == jnp.arange(n_dev, dtype=jnp.int32)[None, None, :]
-        own_has = jnp.any(one_hot, axis=1)
-        own_gate = jnp.sum(jnp.where(one_hot, gate_loc.astype(F32)[:, :, None], 0.0), axis=1)
-        rank = jnp.where(own_has, dot(tri, own_has.astype(BF16), CONTRACT_FIRST) - 1.0, -1.0)
-        col = jnp.arange(n_rows, dtype=jnp.int32)
-        widen = (jnp.arange(n_dev)[:, None] == col[None, :] // slot_cap).astype(BF16)
-        back_match = dot(rank.astype(BF16), widen) == (col % slot_cap).astype(F32)[None, :]
-        back_ones = back_match.astype(BF16)
-        back_gates = jnp.where(back_match, dot(own_gate.astype(BF16), widen), 0.0).astype(BF16)
+        plane = n_dev // n_z
+        my_z, my_p = me // plane, me % plane
+        groups = [[g * plane + i for i in range(plane)] for g in range(n_z)]
+        col = jnp.arange(plane * slot_cap, dtype=jnp.int32)
+        widen = (jnp.arange(plane)[:, None] == col[None, :] // slot_cap).astype(BF16)
+        plane_ids = (my_z * plane + jnp.arange(plane)).astype(F32)
 
-        def give_back(rows):
-            return lax.all_to_all(rows.astype(BF16), 'ep', 0, 0, tiled=True)
+        def pickers(k):
+            other = lax.dynamic_index_in_dim(meta_all, lax.rem(my_z + k, n_z) * plane + my_p, 0, keepdims=False)
+            one_hot = other[:top_k, :, None] == plane_ids[None, None, :]
+            chosen = jnp.any(one_hot, axis=0)
+            weight = jnp.sum(jnp.where(one_hot, other[top_k:, :, None], 0.0), axis=0)
+            rank = jnp.where(chosen, dot(tri, chosen.astype(BF16), CONTRACT_FIRST) - 1.0, -1.0)
+            hit = dot(rank.astype(BF16), widen) == (col % slot_cap).astype(F32)[None, :]
+            return jnp.where(hit, dot(weight.astype(BF16), widen), 0.0).astype(BF16), hit.astype(BF16)
+
+        picks = {k: pickers(k) for k in shifts}
+
+        def go_home(rows, which, before):
+            rows = rows.reshape(n_z, plane * slot_cap, d_model)
+            sums = []
+            for k in shifts:
+                part = lax.dynamic_index_in_dim(rows, lax.rem(my_z + k, n_z), 0, keepdims=False)
+                if before is not None:
+                    part, before = lax.optimization_barrier((part, before))
+                before = lax.all_to_all(part, 'ep', 0, 0, axis_index_groups=groups, tiled=True)
+                sums.append(dot(picks[k][which], before))
+                if k:
+                    sums[-1] = lax.ppermute(sums[-1], 'ep', [(d, (d + k * plane) % n_dev) for d in range(n_dev)])
+            return sums[0] + sums[1] + sums[2] + sums[3], before
 
         wg, wu, wd = w_gate[0], w_up[0], w_down[0]
         x_rows = pick_rows(match, x_all)
@@ -125,7 +145,7 @@
         hidden = (silu_parts(u_val)[0] * v_val).astype(BF16)
         hidden, u_val, v_val = lax.optimization_barrier((hidden, u_val, v_val))
         o_rows = dot(hidden, wd).astype(BF16)
-        back_o = give_back(o_rows)
+        y_reg, o_last = go_home(o_rows, 0, None)
         gate_late, _ = lax.optimization_barrier((gate_mine, o_rows))
 
         q_rows = pick_rows(jnp.where(match, gate_late[:, None, :], 0.0), dy_all)
@@ -134,8 +154,7 @@
         du = (p_val * v_val * silu_grad).astype(BF16)
         dv = (p_val * silu_val).astype(BF16)
         r_rows = (dot(du, wg, CONTRACT_LAST) + dot(dv, wu, CONTRACT_LAST)).astype(BF16)
-        r_rows, back_o = lax.optimization_barrier((r_rows, back_o))
-        back_r = give_back(r_rows)
+        dx_reg, _ = go_home(r_rows, 1, o_last)
         grad_gate = dot(x_rows, du, CONTRACT_FIRST)
         grad_up = dot(x_rows, dv, CONTRACT_FIRST)
         grad_down = dot(hidden, q_rows, CONTRACT_FIRST)
@@ -162,8 +181,8 @@
         hot_dup = dgu[128:128 + part].T
         hot_ddown = dd[:part]
 
-        y_loc = dot(back_gates, back_o) + y_hot
-        dx_loc = dot(back_ones, back_r) + h_r.astype(F32)
+        y_loc = y_reg + y_hot
+        dx_loc = dx_reg + h_r.astype(F32)
         return (y_loc.astype(BF16), dx_loc.astype(BF16), grad_gate[None], grad_up[None], grad_down[None],
                 hot_dgate, hot_dup, hot_ddown)
 

time: 1700 us -> 1580 us (0.929)
  the two profiles are of different devices: /device:TPU:6 before, /device:TPU:11 now
where the time goes in v1:
time: 1580 us
  waiting for transfers between devices  797 us (50%)
  matrix products  478 us (30%)
  starting transfers between devices  127 us (8%)
  Pallas kernels  58.1 us (4%)
  local copies, waits for them, and re-layouts  57.1 us (4%)
  blocking collectives  37.5 us (2%)
    dot_general x28, matrix products, dot(): return lax.dot_general(a, b, dims, preferred_element_type=F32)  424 us
    ppermute x6, waiting for transfers between devices, go_home(): lax.ppermute(sums[-1], 'ep', [(d, (d + k * plane) % n_dev) for d in range...  341 us
    all_gather x1, waiting for transfers between devices, local_step(): x_all = lax.all_gather(x_loc, 'ep', tiled=True)  238 us
    all_to_all x8, waiting for transfers between devices, go_home(): lax.all_to_all(part, 'ep', 0, 0, axis_index_groups=groups, tiled=True)  185 us
    ppermute x6, starting transfers between devices, go_home(): lax.ppermute(sums[-1], 'ep', [(d, (d + k * plane) % n_dev) for d in range...  77.9 us
    pallas_call x1, Pallas kernels, hot_grads(): pl.pallas_call(hot_grad_kernel, grid=(total // block,), in_specs=[pl.Bloc...  58.1 us
    dot_general x2, matrix products, pick_rows(): lax.dot_general(picker.astype(BF16), rows.reshape(n_dev, tok, d_model), (...  54.2 us
    all_to_all x8, starting transfers between devices, go_home(): lax.all_to_all(part, 'ep', 0, 0, axis_index_groups=groups, tiled=True)  49.5 us
  transfers between devices with their start and end apart: 16, of which 12 were waited for; matrix products, arithmetic and copies ran while one was open for 34% of the time, Pallas kernels for 4%

profile of v1, /device:TPU:11, one launch (start us, length us, event | category | flops | bytes accessed | tf_op | source)
XLA Modules:
  0.0 1575.4 jit_solution(10014052740705167008)
XLA Ops:
  10.1 37.5 %all-gather = f32[512,384]{1,0:T(8,128)S(1)} all-gather(f32[16,384]{1,0:T(8,128)S(1)} %pad_maximum_fusion), channel_id=2, replica_groups=mesh['ep'=32] {'ep'}, dimensions={0}, use_global_device_ids=true | all-gather | bytes 811008 | tf_op jit(solution)/shard_map/all_gather | solution.py:87
  49.8 238.2 %all-gather.4.cloned.1.call-done.x_ref = bf16[12288,2048]{1,0:T(8,128)(2,1)} async-done(((bf16[384,2048]{1,0:T(8,128)(2,1)}), bf16[12288,2048]{1,0:T(8,128)(2,1)}) %all-gather.4.cloned.1.call-update) | async-done | bytes 50331664 | tf_op jit(solution)/shard_map/all_gather | solution.py:88
  288.0 27.3 %convolution_convert_fusion.1 = bf16[32,192,2048]{2,1,0:T(8,128)(2,1)} fusion(bf16[32,384,2048]{2,1,0:T(8,128)(2,1)} %bitcast.137, f32[32,384]{1,0:T(8,128)S(1)} %convolution_select_fusion.4, f32[192]{0:T(256)S(1)} %add_convert_fusion.4), kind=kOutput, calls=%fused_computation.9 | convolution fusion | flops 9678618624 | bytes 75547392 | tf_op jit(solution)/shard_map/dot_general | solution.py:100
  315.3 33.0 %fusion.19 = f32[6144,1024]{1,0:T(8,128)} fusion(bf16[6144,2048]{1,0:T(8,128)(2,1)} %bitcast.139, bf16[1,2048,1024]{2,1,0:T(8,128)(2,1)} %param.14), kind=kOutput, calls=%fused_computation.38 | convolution fusion | flops 25769803776 | bytes 54525952 | tf_op jit(solution)/shard_map/dot_general | solution.py:16
  348.3 39.8 %multiply_convert_fusion = (bf16[6144,1024]{1,0:T(8,128)(2,1)}, f32[6144,1024]{1,0:T(8,128)}) fusion(f32[6144,1024]{1,0:T(8,128)} %fusion.19, bf16[6144,2048]{1,0:T(8,128)(2,1)} %bitcast.140, bf16[1,2048,1024]{2,1,0:T(8,128)(2,1)} %param.15), kind=kOutput, calls=%fused_computation.7 | convolution fusion | flops 25807552512 | bytes 92274688 | tf_op jit(solution)/shard_map/dot_general | solution.py:16
  388.1 34.8 %convolution_convert_fusion = bf16[6144,2048]{1,0:T(8,128)(2,1)} fusion(bf16[6144,1024]{1,0:T(8,128)(2,1)} %get-tuple-element.21, bf16[1,1024,2048]{2,1,0:T(8,128)(2,1)S(1)} %copy-done.34), kind=kOutput, calls=%fused_computation.8 | convolution fusion | flops 25782386688 | bytes 41943040 | tf_op jit(solution)/shard_map/dot_general | solution.py:16
  422.9 21.2 %constant_dynamic-slice_fusion.3 = (bf16[1,1536,2048]{2,1,0:T(8,128)(2,1)}, bf16[1536,2048]{1,0:T(8,128)(2,1)}, bf16[1536,2048]{1,0:T(8,128)(2,1)}, bf16[1536,2048]{1,0:T(8,128)(2,1)}) fusion(bf16[4,1536,2048]{2,1,0:T(8,128)(2,1)} %bitcast.144, s32[]{:T(128)S(6)} %select_n.169, s32[]{:T(128)S(6)} %select_n.184, s32[]{:T(128)S(6)} %select_n.179, ...), kind=kLoop, calls=%fused_computation.168 | loop fusion | bytes 50331664 | tf_op jit(solution)/shard_map/jit(dynamic_index_in_dim)/dynamic_slice | solution.py:132
  444.1 5.2 all-to-all-start
  449.5 4.0 copy.25
  453.5 4.0 copy.23
  457.6 0.9 constant_dynamic-slice_fusion
  459.1 118.6 %all-to-all-done = bf16[8,192,2048]{2,1,0:T(8,128)(2,1)} async-done(((bf16[8,192,2048]{2,1,0:T(8,128)(2,1)}), bf16[8,192,2048]{2,1,0:T(8,128)(2,1)}, u32[]{:S(2)}, u32[]{:S(2)}) %all-to-all-start) | async-done | bytes 6291488 | tf_op jit(solution)/shard_map/all_to_all | solution.py:135
  577.6 8.8 all-to-all-start.1
  588.8 1.5 convolution_compare_fusion.2
  590.3 1.5 convolution_compare_fusion.1
  591.8 1.5 convolution_compare_fusion
  593.2 1.5 convolution_compare_fusion.3
  594.8 1.7 constant_dynamic-slice_fusion.1
  597.3 3.0 fusion.118
  600.3 31.0 %all-gather.6.cloned.1.call-done.dy_ref = bf16[12288,2048]{1,0:T(8,128)(2,1)} async-done(((bf16[384,2048]{1,0:T(8,128)(2,1)}), bf16[12288,2048]{1,0:T(8,128)(2,1)}) %all-gather.6.cloned.1.call-update) | async-done | bytes 50331664 | tf_op jit(solution)/shard_map/all_gather | solution.py:89
  631.2 26.9 %convolution_convert_fusion.2 = bf16[32,192,2048]{2,1,0:T(8,128)(2,1)} fusion(bf16[32,384,2048]{2,1,0:T(8,128)(2,1)} %bitcast.138, bf16[32,384]{1,0:T(8,128)(2,1)S(1)} %copy-done.16, f32[32,384]{1,0:T(8,128)S(1)} %copy-done.14, f32[192]{0:T(256)S(1)} %copy-done.18), kind=kOutput, calls=%fused_computation.10 | convolution fusion | flops 9680977920 | bytes 75571968 | tf_op jit(solution)/shard_map/dot_general | solution.py:100
  658.2 4.9 all-to-all-start.2
  663.0 42.9 %fusion.1 = (bf16[6144,1024]{1,0:T(8,128)(2,1)}, bf16[6144,1024]{1,0:T(8,128)(2,1)}) fusion(f32[6144,1024]{1,0:T(8,128)} %get-tuple-element.26, f32[6144,1024]{1,0:T(8,128)} %fusion.19, bf16[6144,2048]{1,0:T(8,128)(2,1)} %bitcast.153, bf16[1,1024,2048]{2,1,0:T(8,128)(2,1)} %param.16), kind=kOutput, calls=%fused_computation.4 | convolution fusion | flops 25845301248 | bytes 104857600 | tf_op jit(solution)/shard_map/dot_general | solution.py:16
  706.0 34.7 %fusion.17 = f32[6144,2048]{1,0:T(8,128)} fusion(bf16[6144,1024]{1,0:T(8,128)(2,1)} %get-tuple-element.69, bf16[1,2048,1024]{2,1,0:T(8,128)(2,1)} %param.14), kind=kOutput, calls=%fused_computation.36 | convolution fusion | flops 25769803776 | bytes 67108864 | tf_op jit(solution)/shard_map/dot_general | solution.py:16
  740.7 4.9 all-to-all-start.3
  745.6 45.1 %add_convert_fusion = bf16[6144,2048]{1,0:T(8,128)(2,1)} fusion(f32[6144,2048]{1,0:T(8,128)} %fusion.17, bf16[1,2048,1024]{2,1,0:T(8,128)(2,1)} %param.15, bf16[6144,1024]{1,0:T(8,128)(2,1)} %get-tuple-element.70, f32[6144,1024]{1,0:T(8,128)} %fusion.19), kind=kOutput, calls=%fused_computation | convolution fusion | flops 25839009792 | bytes 117440512 | tf_op jit(solution)/shard_map/dot_general | solution.py:16
  790.7 18.1 %dynamic-slice_bitcast_fusion.3 = (bf16[1536,2048]{1,0:T(8,128)(2,1)}, bf16[1536,2048]{1,0:T(8,128)(2,1)}, bf16[1536,2048]{1,0:T(8,128)(2,1)}, bf16[1536,2048]{1,0:T(8,128)(2,1)}) fusion(bf16[4,1536,2048]{2,1,0:T(8,128)(2,1)} %bitcast.143, s32[]{:T(128)S(6)} %select_n.169, s32[]{:T(128)S(6)} %select_n.184, s32[]{:T(128)S(6)} %select_n.179, s32[]{:T(128)S(6)} %select_n.174), kind=kLoop, calls=%fused_computation.18 | loop fusion | bytes 50331664 | tf_op jit(solution)/shard_map/jit(dynamic_index_in_dim)/squeeze | solution.py:132
  808.8 6.8 all-to-all-done.3
  815.6 6.4 all-to-all-start.4
  822.0 4.1 fusion.119
  826.2 1.9 fusion.35
  829.7 3.7 fusion.54
  833.4 1.3 slice-done.2
  834.7 31.0 %convolution_bitcast_fusion = f32[1,1024,2048]{2,1,0:T(8,128)} fusion(bf16[6144,1024]{1,0:T(8,128)(2,1)S(1)} %bitcast.164, bf16[6144,2048]{1,0:T(8,128)(2,1)} %bitcast.154), kind=kOutput, calls=%fused_computation.28 | convolution fusion | flops 25769803776 | bytes 46137344 | tf_op jit(solution)/shard_map/dot_general | solution.py:16
  865.7 26.4 %all-to-all-done.4 = bf16[8,192,2048]{2,1,0:T(8,128)(2,1)} async-done(((bf16[8,192,2048]{2,1,0:T(8,128)(2,1)}), bf16[8,192,2048]{2,1,0:T(8,128)(2,1)}, u32[]{:S(2)}, u32[]{:S(2)}) %all-to-all-start.4) | async-done | bytes 6291488 | tf_op jit(solution)/shard_map/all_to_all | solution.py:135
  892.1 6.7 all-to-all-start.5
  898.8 36.8 %convolution_bitcast_fusion.1 = f32[1,2048,1024]{2,1,0:T(8,128)} fusion(bf16[6144,2048]{1,0:T(8,128)(2,1)} %bitcast.141, bf16[6144,1024]{1,0:T(8,128)(2,1)} %get-tuple-element.70, f32[6144,1024]{1,0:T(8,128)} %fusion.19), kind=kOutput, calls=%fused_computation.29 | convolution fusion | flops 25813843968 | bytes 71303168 | tf_op jit(solution)/shard_map/dot_general | solution.py:16
  935.6 33.3 %all-to-all-done.5 = bf16[8,192,2048]{2,1,0:T(8,128)(2,1)} async-done(((bf16[8,192,2048]{2,1,0:T(8,128)(2,1)}), bf16[8,192,2048]{2,1,0:T(8,128)(2,1)}, u32[]{:S(2)}, u32[]{:S(2)}) %all-to-all-start.5) | async-done | bytes 6291488 | tf_op jit(solution)/shard_map/all_to_all | solution.py:135
  968.8 6.5 all-to-all-start.6
  975.3 34.5 %convolution_bitcast_fusion.2 = f32[1,2048,1024]{2,1,0:T(8,128)} fusion(bf16[6144,2048]{1,0:T(8,128)(2,1)} %bitcast.142, bf16[6144,1024]{1,0:T(8,128)(2,1)} %get-tuple-element.69), kind=kOutput, calls=%fused_computation.30 | convolution fusion | flops 25769803776 | bytes 46137344 | tf_op jit(solution)/shard_map/dot_general | solution.py:16
  1009.9 7.5 fusion.39
  1017.4 2.1 collective-permute-start
  1019.5 7.5 fusion.38
  1027.3 7.4 fusion.37
  1034.7 1.3 collective-permute-start.2
  1036.0 7.2 fusion.120
  1043.2 1.1 collective-permute-start.3
  1044.3 7.0 fusion.121
  1051.3 2.3 collective-permute-start.4
  1053.7 6.1 all-to-all-start.7
  1059.8 7.0 fusion.122
  1066.8 88.1 %collective-permute-done = f32[384,2048]{1,0:T(8,128)} collective-permute-done((f32[384,2048]{1,0:T(8,128)}, f32[384,2048]{1,0:T(8,128)}, u32[]{:S(2)}, u32[]{:S(2)}) %collective-permute-start) | collective-permute-done | bytes 3145760 | tf_op jit(solution)/shard_map/ppermute | solution.py:138
  1154.9 70.7 %collective-permute-start.5 = (f32[384,2048]{1,0:T(8,128)}, f32[384,2048]{1,0:T(8,128)}, u32[]{:S(2)}, u32[]{:S(2)}) collective-permute-start(f32[384,2048]{1,0:T(8,128)} %fusion.122), channel_id=1, source_target_pairs={{0,24},{1,25},{2,26},{3,27},{4,28},{5,29},{6,30},{7,31},{8,0},{9,1... | collective-permute-start | bytes 9437192 | tf_op jit(solution)/shard_map/ppermute | solution.py:138
  1225.7 58.1 %hot_grads.1 = (f32[256,2048]{1,0:T(8,128)}, f32[128,2048]{1,0:T(8,128)S(1)}) custom-call(bf16[12288,2048]{1,0:T(8,128)(2,1)} %all-gather.4.cloned.1.call-done.x_ref, bf16[12288,2048]{1,0:T(8,128)(2,1)} %all-gather.6.cloned.1.call-done.dy_ref, f32[12288,1]{1,0:T(8,128)} %bitcast.156, f32[12288,1]{1,0:T(8,128)} %bitcast.155, ...), custom_call_target="tpu_custom_call" | custom-call | flops 38654705664 | bytes 100663296 | tf_op jit(solution)/shard_map/hot_grads/pallas_call | solution.py:50
  1284.4 1.9 slice_bitcast_fusion
  1286.3 7.8 fusion.36
  1294.1 63.0 %collective-permute-done.1 = f32[384,2048]{1,0:T(8,128)} collective-permute-done((f32[384,2048]{1,0:T(8,128)}, f32[384,2048]{1,0:T(8,128)}, u32[]{:S(2)}, u32[]{:S(2)}) %collective-permute-start.1) | collective-permute-done | bytes 3145760 | tf_op jit(solution)/shard_map/ppermute | solution.py:138
  1357.1 68.6 %collective-permute-done.2 = f32[384,2048]{1,0:T(8,128)} collective-permute-done((f32[384,2048]{1,0:T(8,128)}, f32[384,2048]{1,0:T(8,128)}, u32[]{:S(2)}, u32[]{:S(2)}) %collective-permute-start.2) | collective-permute-done | bytes 3145760 | tf_op jit(solution)/shard_map/ppermute | solution.py:138
  1425.8 8.4 add_convert_fusion.3
  1434.2 5.0 fusion.123
  1439.2 52.8 %collective-permute-done.3 = f32[384,2048]{1,0:T(8,128)} collective-permute-done((f32[384,2048]{1,0:T(8,128)}, f32[384,2048]{1,0:T(8,128)}, u32[]{:S(2)}, u32[]{:S(2)}) %collective-permute-start.3) | collective-permute-done | bytes 3145760 | tf_op jit(solution)/shard_map/ppermute | solution.py:138
  1492.0 67.4 %collective-permute-done.4 = f32[384,2048]{1,0:T(8,128)} collective-permute-done((f32[384,2048]{1,0:T(8,128)}, f32[384,2048]{1,0:T(8,128)}, u32[]{:S(2)}, u32[]{:S(2)}) %collective-permute-start.4) | collective-permute-done | bytes 3145760 | tf_op jit(solution)/shard_map/ppermute | solution.py:138
  1559.4 1.2 collective-permute-done.5
  1560.6 7.6 add_convert_fusion.1
  (112 shorter events, 11.5 us)
Async XLA Ops:
  7.2 280.8 %all-gather.4.cloned.1.call-start = ((), (), s32[]{:S(2)}) async-start(), calls=%async_computation.8 | async-start | bytes 51904512 | tf_op jit(solution)/shard_map/all_gather | solution.py:88
  7.9 623.3 %all-gather.6.cloned.1.call-start = ((), (), s32[]{:S(2)}) async-start(), calls=%async_computation.9 | async-start | bytes 51904512 | tf_op jit(solution)/shard_map/all_gather | solution.py:89
  47.6 0.9 copy-start.2
  49.6 265.7 %copy-start.17 = (f32[192]{0:T(256)}, f32[192]{0:T(256)S(1)}, u32[]{:S(2)}) copy-start(f32[192]{0:T(256)S(1)} %add_convert_fusion.4) | copy-start | bytes 2308
  49.7 265.5 %copy-start.13 = (f32[32,384]{1,0:T(8,128)}, f32[32,384]{1,0:T(8,128)S(1)}, u32[]{:S(2)}) copy-start(f32[32,384]{1,0:T(8,128)S(1)} %convolution_select_fusion.4) | copy-start | bytes 147460
  348.3 39.8 %copy-start.34 = (bf16[1,1024,2048]{2,1,0:T(8,128)(2,1)S(1)}, bf16[1,1024,2048]{2,1,0:T(8,128)(2,1)}, u32[]{:S(2)}) copy-start(bf16[1,1024,2048]{2,1,0:T(8,128)(2,1)} %param.16) | copy-start | bytes 12582916
  444.1 5.2 copy-start.15
  444.1 5.3 copy-start.22
  444.1 133.5 %all-to-all-start = ((bf16[8,192,2048]{2,1,0:T(8,128)(2,1)}), bf16[8,192,2048]{2,1,0:T(8,128)(2,1)}, u32[]{:S(2)}, u32[]{:S(2)}) async-start(bf16[8,192,2048]{2,1,0:T(8,128)(2,1)} %bitcast.149), calls=%async_computation | async-start | bytes 12582912 | tf_op jit(solution)/shard_map/all_to_all | solution.py:135
  453.5 5.0 copy-start.21
  458.5 134.7 %copy-start.26 = (s32[1536]{0:T(1024)}, s32[1536]{0:T(1024)S(1)}, u32[]{:S(2)}) copy-start(s32[1536]{0:T(1024)S(1)} %get-tuple-element.71) | copy-start | bytes 18436
  577.6 8.9 copy-start.23
  577.6 80.5 %all-to-all-start.1 = ((bf16[8,192,2048]{2,1,0:T(8,128)(2,1)}), bf16[8,192,2048]{2,1,0:T(8,128)(2,1)}, u32[]{:S(2)}, u32[]{:S(2)}) async-start(bf16[8,192,2048]{2,1,0:T(8,128)(2,1)} %bitcast.147), calls=%async_computation.1 | async-start | bytes 12582912 | tf_op jit(solution)/shard_map/all_to_all | solution.py:135
  593.2 3.5 copy-start.8
  594.8 2.5 copy-start.19
  597.3 33.9 %copy-start.14 = (f32[32,384]{1,0:T(8,128)S(1)}, f32[32,384]{1,0:T(8,128)}, u32[]{:S(2)}) copy-start(f32[32,384]{1,0:T(8,128)} %copy-done.13) | copy-start | bytes 147460
  597.3 33.9 %copy-start.16 = (bf16[32,384]{1,0:T(8,128)(2,1)S(1)}, bf16[32,384]{1,0:T(8,128)(2,1)}, u32[]{:S(2)}) copy-start(bf16[32,384]{1,0:T(8,128)(2,1)} %get-tuple-element.25) | copy-start | bytes 73732
  597.3 33.9 %copy-start.18 = (f32[192]{0:T(256)S(1)}, f32[192]{0:T(256)}, u32[]{:S(2)}) copy-start(f32[192]{0:T(256)} %copy-done.17) | copy-start | bytes 2308
  658.2 82.5 %all-to-all-start.2 = ((bf16[8,192,2048]{2,1,0:T(8,128)(2,1)}), bf16[8,192,2048]{2,1,0:T(8,128)(2,1)}, u32[]{:S(2)}, u32[]{:S(2)}) async-start(bf16[8,192,2048]{2,1,0:T(8,128)(2,1)} %bitcast.146), calls=%async_computation.2 | async-start | bytes 12582912 | tf_op jit(solution)/shard_map/all_to_all | solution.py:135
  740.7 75.0 %all-to-all-start.3 = ((bf16[8,192,2048]{2,1,0:T(8,128)(2,1)}), bf16[8,192,2048]{2,1,0:T(8,128)(2,1)}, u32[]{:S(2)}, u32[]{:S(2)}) async-start(bf16[8,192,2048]{2,1,0:T(8,128)(2,1)} %bitcast.145), calls=%async_computation.3 | async-start | bytes 12582912 | tf_op jit(solution)/shard_map/all_to_all | solution.py:135
  815.6 6.4 copy-start.9
  815.6 76.5 %all-to-all-start.4 = ((bf16[8,192,2048]{2,1,0:T(8,128)(2,1)}), bf16[8,192,2048]{2,1,0:T(8,128)(2,1)}, u32[]{:S(2)}, u32[]{:S(2)}) async-start(bf16[8,192,2048]{2,1,0:T(8,128)(2,1)} %bitcast.152), calls=%async_computation.4 | async-start | bytes 12582912 | tf_op jit(solution)/shard_map/all_to_all | solution.py:135
  822.0 4.2 copy-start.4
  822.0 4.2 copy-start.10
  822.0 4.2 copy-start.24
  826.2 2.0 copy-start.6
  826.2 2.9 copy-start
  826.2 3.5 copy-start.20
  826.2 3.5 copy-start.32
  826.2 7.2 slice-start
  826.2 7.2 slice-start.1
  828.1 0.9 copy-start.11
  829.7 5.0 slice-start.2
  892.1 76.8 %all-to-all-start.5 = ((bf16[8,192,2048]{2,1,0:T(8,128)(2,1)}), bf16[8,192,2048]{2,1,0:T(8,128)(2,1)}, u32[]{:S(2)}, u32[]{:S(2)}) async-start(bf16[8,192,2048]{2,1,0:T(8,128)(2,1)} %bitcast.151), calls=%async_computation.5 | async-start | bytes 12582912 | tf_op jit(solution)/shard_map/all_to_all | solution.py:135
  968.8 84.8 %all-to-all-start.6 = ((bf16[8,192,2048]{2,1,0:T(8,128)(2,1)}), bf16[8,192,2048]{2,1,0:T(8,128)(2,1)}, u32[]{:S(2)}, u32[]{:S(2)}) async-start(bf16[8,192,2048]{2,1,0:T(8,128)(2,1)} %bitcast.150), calls=%async_computation.6 | async-start | bytes 12582912 | tf_op jit(solution)/shard_map/all_to_all | solution.py:135
  975.3 34.5 %copy-start.27 = (s32[1536]{0:T(1024)S(1)}, s32[1536]{0:T(1024)}, u32[]{:S(2)}) copy-start(s32[1536]{0:T(1024)} %copy-done.26) | copy-start | bytes 18436
  975.3 34.5 %copy-start.31 = (bf16[384,8]{0,1:T(8,128)(2,1)S(1)}, bf16[384,8]{0,1:T(8,128)(2,1)}, u32[]{:S(2)}) copy-start(bf16[384,8]{0,1:T(8,128)(2,1)} %get-tuple-element.39) | copy-start | bytes 18436
  975.3 34.5 %copy-start.37 = (pred[384,1536]{1,0:T(32,128)(4,1)S(1)}, pred[384,1536]{1,0:T(32,128)(4,1)}, u32[]{:S(2)}) copy-start(pred[384,1536]{1,0:T(32,128)(4,1)} %convolution_compare_fusion.3) | copy-start | bytes 1769476
  1009.8 9.6 copy-start.30
  1009.8 9.6 copy-start.36
  1017.4 137.5 %collective-permute-start = (f32[384,2048]{1,0:T(8,128)}, f32[384,2048]{1,0:T(8,128)}, u32[]{:S(2)}, u32[]{:S(2)}) collective-permute-start(f32[384,2048]{1,0:T(8,128)} %fusion.39), channel_id=1, source_target_pairs={{0,16},{1,17},{2,18},{3,19},{4,20},{5,21},{6,22},{7,23},{8,24},{9,... | collective-permute-start | bytes 9437192 | tf_op jit(solution)/shard_map/ppermute | solution.py:138
  1019.5 7.8 copy-start.29
  1019.5 7.8 copy-start.35
  1026.9 330.2 %collective-permute-start.1 = (f32[384,2048]{1,0:T(8,128)}, f32[384,2048]{1,0:T(8,128)}, u32[]{:S(2)}, u32[]{:S(2)}) collective-permute-start(f32[384,2048]{1,0:T(8,128)} %fusion.38), channel_id=1, source_target_pairs={{0,8},{1,9},{2,10},{3,11},{4,12},{5,13},{6,14},{7,15},{8,16},{9,17... | collective-permute-start | bytes 9437192 | tf_op jit(solution)/shard_map/ppermute | solution.py:138
  1034.7 391.1 %collective-permute-start.2 = (f32[384,2048]{1,0:T(8,128)}, f32[384,2048]{1,0:T(8,128)}, u32[]{:S(2)}, u32[]{:S(2)}) collective-permute-start(f32[384,2048]{1,0:T(8,128)} %fusion.37), channel_id=1, source_target_pairs={{0,24},{1,25},{2,26},{3,27},{4,28},{5,29},{6,30},{7,31},{8,0},{9,1... | collective-permute-start | bytes 9437192 | tf_op jit(solution)/shard_map/ppermute | solution.py:138
  1043.2 448.7 %collective-permute-start.3 = (f32[384,2048]{1,0:T(8,128)}, f32[384,2048]{1,0:T(8,128)}, u32[]{:S(2)}, u32[]{:S(2)}) collective-permute-start(f32[384,2048]{1,0:T(8,128)} %fusion.120), channel_id=1, source_target_pairs={{0,16},{1,17},{2,18},{3,19},{4,20},{5,21},{6,22},{7,23},{8,24},{9,... | collective-permute-start | bytes 9437192 | tf_op jit(solution)/shard_map/ppermute | solution.py:138
  1051.3 508.1 %collective-permute-start.4 = (f32[384,2048]{1,0:T(8,128)}, f32[384,2048]{1,0:T(8,128)}, u32[]{:S(2)}, u32[]{:S(2)}) collective-permute-start(f32[384,2048]{1,0:T(8,128)} %fusion.121), channel_id=1, source_target_pairs={{0,8},{1,9},{2,10},{3,11},{4,12},{5,13},{6,14},{7,15},{8,16},{9,17... | collective-permute-start | bytes 9437192 | tf_op jit(solution)/shard_map/ppermute | solution.py:138
  1053.7 380.5 %all-to-all-start.7 = ((bf16[8,192,2048]{2,1,0:T(8,128)(2,1)}), bf16[8,192,2048]{2,1,0:T(8,128)(2,1)}, u32[]{:S(2)}, u32[]{:S(2)}) async-start(bf16[8,192,2048]{2,1,0:T(8,128)(2,1)} %bitcast.148), calls=%async_computation.7 | async-start | bytes 12582912 | tf_op jit(solution)/shard_map/all_to_all | solution.py:135
  1154.9 405.7 %collective-permute-start.5 = (f32[384,2048]{1,0:T(8,128)}, f32[384,2048]{1,0:T(8,128)}, u32[]{:S(2)}, u32[]{:S(2)}) collective-permute-start(f32[384,2048]{1,0:T(8,128)} %fusion.122), channel_id=1, source_target_pairs={{0,24},{1,25},{2,26},{3,27},{4,28},{5,29},{6,30},{7,31},{8,0},{9,1... | collective-permute-start | bytes 9437192 | tf_op jit(solution)/shard_map/ppermute | solution.py:138
  1225.6 60.7 %copy-start.28 = (bf16[384,8]{0,1:T(8,128)(2,1)S(1)}, bf16[384,8]{0,1:T(8,128)(2,1)}, u32[]{:S(2)}) copy-start(bf16[384,8]{0,1:T(8,128)(2,1)} %get-tuple-element.37) | copy-start | bytes 18436
  1286.3 139.5 %copy-start.1 = (f32[384,1024]{1,0:T(8,128)S(1)}, f32[384,1024]{1,0:T(8,128)}, u32[]{:S(2)}) copy-start(f32[384,1024]{1,0:T(8,128)} %fusion.118) | copy-start | bytes 4718596
  1286.3 139.5 %copy-start.7 = (f32[384,1024]{1,0:T(8,128)S(1)}, f32[384,1024]{1,0:T(8,128)}, u32[]{:S(2)}) copy-start(f32[384,1024]{1,0:T(8,128)} %copy-done.6) | copy-start | bytes 4718596
  1286.3 139.5 %copy-start.25 = (f32[384]{0:T(512)S(1)}, f32[384]{0:T(512)}, u32[]{:S(2)}) copy-start(f32[384]{0:T(512)} %fusion.83) | copy-start | bytes 4612
  1286.3 139.4 %copy-start.33 = (pred[384]{0:T(512)(128)(4,1)S(1)}, pred[384]{0:T(512)(128)(4,1)}, u32[]{:S(2)}) copy-start(pred[384]{0:T(512)(128)(4,1)} %get-tuple-element.47) | copy-start | bytes 1156
  1434.2 126.4 %copy-start.3 = (bf16[2048,1024]{1,0:T(8,128)(2,1)S(1)}, bf16[2048,1024]{1,0:T(8,128)(2,1)}, u32[]{:S(2)}) copy-start(bf16[2048,1024]{1,0:T(8,128)(2,1)} %param.18) | copy-start | bytes 12582916
  1434.2 126.4 %copy-start.5 = (f32[384,2048]{1,0:T(8,128)S(1)}, f32[384,2048]{1,0:T(8,128)}, u32[]{:S(2)}) copy-start(f32[384,2048]{1,0:T(8,128)} %fusion.54) | copy-start | bytes 9437188
  1434.2 126.4 %copy-start.12 = (bf16[384,1024]{1,0:T(8,128)(2,1)S(1)}, bf16[384,1024]{1,0:T(8,128)(2,1)}, u32[]{:S(2)}) copy-start(bf16[384,1024]{1,0:T(8,128)(2,1)} %copy-done.11) | copy-start | bytes 2359300
Sparse Core Ops, SparseCore 0:
  10.8 277.0 all-gather.3
  290.8 340.3 all-gather.5
